TPU v7x, 32 devices: a whole 2x2x4 slice. The times are simulated.
32 devices in a mesh: row: 8 (over z, core), col: 4 (over y, x).
Axes of the slice: x: 2, y: 2, z: 4, core: 2. Of those that a mesh axis runs over, the one named last changes fastest.
Arguments:
- ancestor_inverse: float32 [12288, 12288], P('row', 'col'), may hold values from -6 to 6
- panel: float32 [5632, 512], P('col', 'row'), may hold values from -0.078125 to 0.078125
- unit_inverse: float32 [512, 512], P('row'), may hold values from -1 to 1, as said below
- pivot_inverse: float32 [512, 512], P('row', 'col'), may hold values from -6 to 6
- panel_blocks: int32 [44], replicated, may hold values from 0 to 95, as said below
Outputs:
- inverse_row: float32 [512, 12288], P('col', 'row')
- diagonal_block: float32 [512, 512], P('row', 'col')
Inputs may be any that keep to these rules, and one draw needn't show every extreme that they name: `panel_blocks`: Distinct, in no particular order. Among the window blocks c * 24 to c * 24 + 23 of any process column c at most 12 are listed, and exactly 12 for some columns. `unit_inverse`: unit lower triangular: ones on the diagonal, zeros above it.
All inputs are finite; a program needn't handle non-finite values.
Results may differ from a plain program's by a relative error of at most 0.00011.
Values sent between devices are 32-bit elements; how exact they have to be, the bound alone decides.
A program may use at most 128 MiB of HBM per device.

v0:
```python
import functools

import jax
import jax.numpy as jnp
from jax import lax
from jax.experimental import pallas as pl
from jax.experimental.pallas import tpu as pltpu
from jax.sharding import PartitionSpec as P

BLK = 128
NT = (((1,), (1,)), ((), ()))


def select_kernel(per_shard, ids_ref, live_ref, gathered_ref, out_ref):
    slots = out_ref.shape[2] // BLK
    for target in range(out_ref.shape[0]):
        for slot in range(slots):
            at = target * slots + slot
            block = ids_ref[at]
            start = pl.multiple_of((block % per_shard) * BLK, BLK)
            value = gathered_ref[block // per_shard, :, pl.ds(start, BLK)]
            out_ref[target, :, slot * BLK : (slot + 1) * BLK] = jnp.where(
                live_ref[at] > 0, value, 0.0
            )


def select(gathered, ids, live, targets):
    slots = ids.shape[0] // targets
    per_shard = gathered.shape[2] // BLK
    smem = pl.BlockSpec(memory_space=pltpu.SMEM)
    vmem = pl.BlockSpec(memory_space=pltpu.VMEM)
    return pl.pallas_call(
        functools.partial(select_kernel, per_shard),
        out_shape=jax.ShapeDtypeStruct((targets, gathered.shape[1], slots * BLK), jnp.float32),
        in_specs=[smem, smem, vmem],
        out_specs=vmem,
    )(ids, live, gathered)


def halves(value):
    high = value.astype(jnp.bfloat16)
    return high, (value - high.astype(jnp.float32)).astype(jnp.bfloat16)


def product_kernel(group, ids_ref, normal_ref, *refs):
    out_ref = refs[group]

    @pl.when(pl.program_id(1) == 0)
    def _():
        out_ref[...] = jnp.zeros_like(out_ref)

    n_high, n_low = halves(normal_ref[...])
    if group == 1:
        block = refs[0][...]
    else:
        block = jnp.concatenate([ref[...] for ref in refs[:group]], axis=1)
    a_high, a_low = halves(block)
    dot = functools.partial(
        lax.dot_general, dimension_numbers=NT, preferred_element_type=jnp.float32
    )
    out_ref[...] -= dot(n_high, a_high) + (dot(n_high, a_low) + dot(n_low, a_high))


def product(normal, ancestor, ids):
    width, slots = normal.shape[0], ids.shape[0]
    rows = ancestor.shape[0]
    group = 2 if slots % 2 == 0 else 1
    tile = 512 if rows % 512 == 0 else BLK

    def column(k):
        return pl.BlockSpec((tile, BLK), lambda i, j, ids: (i, ids[j * group + k]))

    return pl.pallas_call(
        functools.partial(product_kernel, group),
        out_shape=jax.ShapeDtypeStruct((width, rows), jnp.float32),
        grid_spec=pltpu.PrefetchScalarGridSpec(
            num_scalar_prefetch=1,
            grid=(rows // tile, slots // group),
            in_specs=[pl.BlockSpec((width, group * BLK), lambda i, j, ids: (0, j))]
            + [column(k) for k in range(group)],
            out_specs=pl.BlockSpec((width, tile), lambda i, j, ids: (0, i)),
        ),
        compiler_params=pltpu.CompilerParams(
            dimension_semantics=("arbitrary", "arbitrary"), vmem_limit_bytes=32 << 20
        ),
        cost_estimate=pl.CostEstimate(
            flops=6 * width * rows * slots * BLK,
            bytes_accessed=4 * (rows * slots * BLK + 2 * width * rows),
            transcendentals=0,
        ),
    )(ids, normal, *([ancestor] * group))


def on_device(ancestor_inverse, panel, unit_inverse, pivot_inverse, panel_blocks):
    high = lax.Precision.HIGH
    col_index = lax.axis_index("col")
    rows_here, cols_here = ancestor_inverse.shape
    width = unit_inverse.shape[1]
    block_total = panel_blocks.shape[0]
    range_blocks = cols_here // BLK
    row_blocks = rows_here // BLK
    first_block = col_index * range_blocks
    slot_count = range_blocks // 2

    gathered = lax.all_gather(panel.T, "col", axis=0, tiled=False)
    half = width // 2
    unit = [
        lax.all_gather(unit_inverse[:, k * half : (k + 1) * half], "row", axis=0, tiled=True)
        for k in range(2)
    ]

    in_range = (panel_blocks >= first_block) & (panel_blocks < first_block + range_blocks)
    order = jnp.arange(block_total, dtype=jnp.int32)
    upto = order[None, :] <= order[:, None]
    rank_of = jnp.sum((upto & in_range[None, :]).astype(jnp.int32), axis=1) - 1
    slot_ids = jnp.arange(slot_count, dtype=jnp.int32)
    selected = in_range[None, :] & (rank_of[None, :] == slot_ids[:, None])
    stored_ids = jnp.sum(jnp.where(selected, order[None, :], 0), axis=1)
    chosen_ids = jnp.sum(jnp.where(selected, panel_blocks[None, :], 0), axis=1)
    slot_live = jnp.sum(selected.astype(jnp.int32), axis=1)
    local_ids = jnp.clip(chosen_ids - first_block, 0, range_blocks - 1)
    gathered, unit = lax.optimization_barrier((gathered, unit))
    unit = jnp.concatenate(unit, axis=1)
    rows, cols = lax.axis_size("row"), lax.axis_size("col")
    chosen = select(gathered, stored_ids, slot_live, 1)[0]
    window = lax.all_gather(chosen, "row", axis=0, tiled=True)

    match = panel_blocks[None, :] == jnp.arange(rows * row_blocks, dtype=jnp.int32)[:, None]
    block_ids = jnp.sum(jnp.where(match, order[None, :], 0), axis=1)
    block_live = jnp.sum(match.astype(jnp.int32), axis=1)
    part = panel.shape[1] // cols
    share = lax.dynamic_slice_in_dim(gathered, col_index * part, part, 1)
    listed = lax.all_to_all(select(share, block_ids, block_live, rows), "row", 0, 0)
    listed = lax.all_gather(listed, "col", axis=0, tiled=False).reshape(width, rows_here)
    unit_mixed = unit.reshape(rows, cols, part, width).transpose(1, 0, 2, 3).reshape(width, width)

    def normalise(factor, value):
        return lax.dot_general(
            factor,
            value,
            (((0,), (0,)), ((), ())),
            precision=high,
            preferred_element_type=jnp.float32,
        )

    normal = normalise(unit, window)
    own_window = normalise(unit_mixed, listed)
    inverse_tile = lax.psum_scatter(
        product(normal, ancestor_inverse, local_ids), "col", scatter_dimension=0, tiled=True
    )
    crossed = -lax.dot_general(
        own_window, inverse_tile, NT, precision=high, preferred_element_type=jnp.float32
    )
    parts = lax.all_to_all(
        crossed.reshape(width // pivot_inverse.shape[0], *pivot_inverse.shape), "row", 0, 0
    )
    diagonal_block = pivot_inverse + jnp.sum(parts, axis=0)
    return (inverse_tile, diagonal_block)


def solution(mesh):
    return jax.shard_map(
        on_device,
        mesh=mesh,
        in_specs=(P("row", "col"), P("col", "row"), P("row", None), P("row", "col"), P()),
        out_specs=(P("col", "row"), P("row", "col")),
        check_vma=False,
    )
```

profile of v0, /device:TPU:0, one launch (start us, length us, event | category | flops | bytes accessed | tf_op | source)
XLA Modules:
  0.0 216.8 jit_solution(14092006106985666948)
XLA Ops:
  7.2 0.7 all-gather.7.cloned.1.call-update
  8.0 0.7 compare_and_fusion
  8.6 0.1 convert_reduce_fusion.1
  8.7 1.3 convert_reduce_fusion.2
  10.0 0.9 fusion.6
  10.9 16.5 %all_gather.23 = f32[512,256]{1,0:T(8,128)S(1)} all-gather(f32[64,256]{1,0:T(8,128)S(1)} %get-tuple-element.14), channel_id=1, replica_groups=mesh['row'=8,'col'=4] {'row'}, dimensions={0}, use_global_device_ids=true | all-gather | bytes 589824 | tf_op jit(solution)/shard_map/all_gather | solution.py:108
  27.4 14.8 %all_gather.24 = f32[512,256]{1,0:T(8,128)S(1)} all-gather(f32[64,256]{1,0:T(8,128)S(1)} %get-tuple-element.13), channel_id=1, replica_groups=mesh['row'=8,'col'=4] {'row'}, dimensions={0}, use_global_device_ids=true | all-gather | bytes 589824 | tf_op jit(solution)/shard_map/all_gather | solution.py:108
  42.2 0.1 all-gather.7.cloned.1.call-done
  42.3 2.3 %shard_map.68 = f32[1,64,1536]{2,1,0:T(8,128)} custom-call(s32[12]{0:T(128)} %get-tuple-element.9.ids_ref, s32[12]{0:T(128)} %get-tuple-element.8.live_ref, f32[4,64,1408]{2,1,0:T(8,128)} %bitcast.20), custom_call_target="tpu_custom_call" | custom-call | tf_op jit(solution)/shard_map/pallas_call | solution.py:32
  44.7 0.6 convert_reduce_fusion
  45.3 1.7 constant_dynamic-slice_fusion.gathered_ref
  47.1 2.7 %shard_map.70 = f32[8,16,1536]{2,1,0:T(8,128)} custom-call(s32[96]{0:T(128)} %get-tuple-element.12.ids_ref, s32[96]{0:T(128)} %get-tuple-element.11.live_ref, f32[4,16,1408]{2,1,0:T(8,128)} %constant_dynamic-slice_fusion.gathered_ref), custom_call_target="tpu_custom_call" | custom-call | tf_op jit(solution)/shard_map/pallas_call | solution.py:32
  49.8 46.6 %all_to_all.10 = f32[8,16,1536]{2,1,0:T(8,128)} all-to-all(f32[8,16,1536]{2,1,0:T(8,128)} %shard_map.70), channel_id=1, replica_groups=mesh['row'=8,'col'=4] {'row'}, dimensions={0} | all-to-all | bytes 1572864 | tf_op jit(solution)/shard_map/all_to_all | solution.py:133
  96.4 0.1 constant_dynamic-update-slice_fusion.1
  96.5 0.1 constant_dynamic-update-slice_fusion
  96.5 4.5 %all-gather.9.cloned.1.call-done = f32[1,512,1536]{2,1,0:T(8,128)} async-done(((f32[1,64,1536]{2,1,0:T(8,128)}), f32[1,512,1536]{2,1,0:T(8,128)}) %all-gather.9.cloned.1.call-update) | async-done | bytes 3145744 | tf_op jit(solution)/shard_map/all_gather | solution.py:126
  101.1 4.7 %fusion.normal_ref = f32[512,1536]{1,0:T(8,128)S(1)} fusion(f32[512,512]{1,0:T(8,128)S(1)} %constant_dynamic-update-slice_fusion, f32[1,512,1536]{2,1,0:T(8,128)} %all-gather.9.cloned.1.call-done), kind=kOutput, calls=%fused_computation.1 | convolution fusion | flops 2415919104 | bytes 7340032 | tf_op jit(solution)/shard_map/dot_general | solution.py:138
  105.8 18.8 %shard_map.69 = f32[512,1536]{1,0:T(8,128)} custom-call(s32[12]{0:T(128)S(1)} %subtract_clamp_fusion.ids_ref, f32[512,1536]{1,0:T(8,128)S(1)} %fusion.normal_ref, f32[1536,3072]{1,0:T(8,128)} %refs_1_.1, f32[1536,3072]{1,0:T(8,128)} %refs_1_.1), custom_call_target="tpu_custom_call" | custom-call | flops 7247757312 | bytes 15728640 | tf_op jit(solution)/shard_map/pallas_call | solution.py:73
  124.6 21.0 %all-gather.11.cloned.1.call-done = f32[32,16,1536]{2,1,0:T(8,128)} async-done(((f32[8,16,1536]{2,1,0:T(8,128)}), f32[32,16,1536]{2,1,0:T(8,128)}) %all-gather.11.cloned.1.call-update) | async-done | bytes 3145744 | tf_op jit(solution)/shard_map/all_gather | solution.py:134
  145.6 5.0 %convolution_bitcast_fusion = f32[512,1536]{1,0:T(8,128)S(1)} fusion(f32[4,8,16,1536]{3,2,1,0:T(8,128)} %bitcast.24, f32[8,4,16,512]{3,2,1,0:T(8,128)} %bitcast.19), kind=kOutput, calls=%fused_computation | convolution fusion | flops 2415919104 | bytes 7340032 | tf_op jit(solution)/shard_map/dot_general | solution.py:138
  150.6 42.4 %reduce-scatter.2.cloned.1.call-done = f32[128,1536]{1,0:T(8,128)} async-done(((f32[512,1536]{1,0:T(8,128)}), f32[128,1536]{1,0:T(8,128)}) %reduce-scatter.2.cloned.1.call-update) | async-done | bytes 786448 | tf_op jit(solution)/shard_map/reduce_scatter | solution.py:148
  193.0 2.5 %convolution_negate_fusion = f32[512,128]{1,0:T(8,128)S(1)} fusion(f32[512,1536]{1,0:T(8,128)S(1)} %convolution_bitcast_fusion, f32[128,1536]{1,0:T(8,128)} %reduce-scatter.2.cloned.1.call-done), kind=kOutput, calls=%fused_computation.3 | convolution fusion | flops 604045312 | bytes 4194304 | tf_op jit(solution)/shard_map/dot_general | solution.py:151
  195.5 14.1 %all_to_all.11 = f32[8,64,128]{2,1,0:T(8,128)S(1)} all-to-all(f32[8,64,128]{2,1,0:T(8,128)S(1)} %bitcast.22), channel_id=1, replica_groups=mesh['row'=8,'col'=4] {'row'}, dimensions={0} | all-to-all | bytes 524288 | tf_op jit(solution)/shard_map/all_to_all | solution.py:154
  209.6 0.6 add.18
  (16 shorter events, 0.3 us)
Async XLA Ops:
  7.2 37.5 %copy-start.2 = (s32[44]{0:T(128)S(1)}, s32[44]{0:T(128)}, u32[]{:S(2)}) copy-start(s32[44]{0:T(128)} %param.9) | copy-start | bytes 532
  7.2 35.2 %all-gather.7.cloned.1.call-start = ((), (), s32[]{:S(2)}) async-start(), calls=%async_computation.4 | async-start | bytes 1802240 | tf_op jit(solution)/shard_map/all_gather | solution.py:105
  7.9 93.2 %all-gather.9.cloned.1.call-start = ((), (), s32[]{:S(2)}) async-start(), calls=%async_computation.5 | async-start | bytes 3538944 | tf_op jit(solution)/shard_map/all_gather | solution.py:126
  44.6 101.0 %all-gather.11.cloned.1.call-start = ((), (), s32[]{:S(2)}) async-start(), calls=%async_computation.6 | async-start | bytes 3932160 | tf_op jit(solution)/shard_map/all_gather | solution.py:134
  96.3 96.6 %reduce-scatter.2.cloned.1.call-start = ((), (), s32[]{:S(2)}) async-start(), calls=%async_computation.3 | async-start | bytes 3932160 | tf_op jit(solution)/shard_map/reduce_scatter | solution.py:148
  96.5 9.3 %copy-start = (f32[512,512]{1,0:T(8,128)}, f32[512,512]{1,0:T(8,128)S(1)}, u32[]{:S(2)}) copy-start(f32[512,512]{1,0:T(8,128)S(1)} %constant_dynamic-update-slice_fusion) | copy-start | bytes 3145732
  150.6 59.0 %copy-start.1 = (f32[64,128]{1,0:T(8,128)S(1)}, f32[64,128]{1,0:T(8,128)}, u32[]{:S(2)}) copy-start(f32[64,128]{1,0:T(8,128)} %param.8) | copy-start | bytes 98308
Sparse Core Ops, SparseCore 0:
  9.8 32.4 all-gather.6
  44.7 56.3 all-gather.8
  102.9 42.6 all-gather.10
  149.0 43.8 reduce-scatter.1
where the time goes:
time: 218 us; the launch traced here: 217 us
  blocking collectives  92 us (42%)
  waiting for transfers between devices  68.8 us (32%)
  Pallas kernels  23.7 us (11%)
  between operations  13.9 us (6%)
  matrix products  12.2 us (6%)
  other arithmetic  3.35 us (2%)
  local copies, waits for them, and re-layouts  2.74 us (1%)
    all_to_all x1, blocking collectives, on_device(): lax.all_to_all(select(share, block_ids, block_live, rows), 'row', 0, 0)  46.6 us
    reduce_scatter x1, waiting for transfers between devices, on_device(): lax.psum_scatter(product(normal, ancestor_inverse, local_ids), 'col', sca...  42.4 us
    all_gather x2, blocking collectives, on_device(): lax.all_gather(unit_inverse[:, k * half:(k + 1) * half], 'row', axis=0, t...  31.3 us
    all_gather x1, waiting for transfers between devices, on_device(): lax.all_gather(listed, 'col', axis=0, tiled=False).reshape(width, rows_here)  21 us
    pallas_call x1, Pallas kernels, product(): pl.pallas_call(functools.partial(product_kernel, group), out_shape=jax.Sh...  18.8 us
    all_to_all x1, blocking collectives, on_device(): lax.all_to_all(crossed.reshape(width // pivot_inverse.shape[0], *pivot_in...  14.1 us
    dot_general x2, matrix products, normalise(): lax.dot_general(factor, value, (((0,), (0,)), ((), ())), precision=high,...  9.67 us
    pallas_call x2, Pallas kernels, select(): pl.pallas_call(functools.partial(select_kernel, per_shard), out_shape=jax...  4.96 us
  transfers between devices with their start and end apart: 4, of which 4 were waited for; matrix products, arithmetic and copies ran while one was open for 7% of the time, Pallas kernels for 10%

commit v1 on v0

--- a/solution.py
+++ b/solution.py
@@ -9,6 +9,8 @@
 
 BLK = 128
 NT = (((1,), (1,)), ((), ()))
+NN = (((1,), (0,)), ((), ()))
+MESH = pl.DeviceIdType.MESH
 
 
 def select_kernel(per_shard, ids_ref, live_ref, gathered_ref, out_ref):
@@ -158,11 +160,526 @@
     return (inverse_tile, diagonal_block)
 
 
+def table_kernel(cols, range_blocks, row_blocks, per_shard, ids_ref, slot_ref, block_ref, live_ref):
+    c = lax.axis_index("col")
+    slots = slot_ref.shape[1]
+    quarter = row_blocks // cols
+    for at in range(slots):
+        for field in range(3):
+            slot_ref[field, at] = 0
+    for at in range(block_ref.shape[1]):
+        for field in range(2):
+            block_ref[field, at] = 0
+    for at in range(live_ref.shape[0]):
+        live_ref[at] = 0.0
+
+    def step(k, rank):
+        block = ids_ref[k]
+        shard = k // per_shard
+        offset = k % per_shard
+        local = block - c * range_blocks
+        here = (local >= 0) & (local < range_blocks)
+
+        @pl.when(here)
+        def _():
+            slot_ref[0, rank] = shard
+            slot_ref[1, rank] = offset
+            slot_ref[2, rank] = local
+            live_ref[rank] = 1.0
+
+        row = block // row_blocks
+        within = block % row_blocks
+
+        @pl.when(within // quarter == c)
+        def _():
+            at = row * quarter + within % quarter
+            block_ref[0, at] = shard
+            block_ref[1, at] = offset
+            live_ref[slots + at] = 1.0
+
+        return rank + here.astype(jnp.int32)
+
+    lax.fori_loop(0, ids_ref.shape[0], step, jnp.int32(0))
+
+
+def tables(ids, cols, range_blocks, row_blocks, rows):
+    smem = pl.BlockSpec(memory_space=pltpu.SMEM)
+    quarter = row_blocks // cols
+    return pl.pallas_call(
+        functools.partial(
+            table_kernel, cols, range_blocks, row_blocks, ids.shape[0] // cols
+        ),
+        out_shape=(
+            jax.ShapeDtypeStruct((3, range_blocks // 2), jnp.int32),
+            jax.ShapeDtypeStruct((2, rows * quarter), jnp.int32),
+            jax.ShapeDtypeStruct((range_blocks // 2 + rows * quarter,), jnp.float32),
+        ),
+        in_specs=[smem],
+        out_specs=(smem, smem, smem),
+    )(ids)
+
+
+def dot(a, b, dims):
+    return lax.dot_general(a, b, dims, preferred_element_type=jnp.float32)
+
+
+def dot3(a, b, dims):
+    a_high, a_low = a
+    b_high, b_low = b
+    return dot(a_high, b_high, dims) + (dot(a_high, b_low, dims) + dot(a_low, b_high, dims))
+
+
+PARTS = 4
+A_TILES = 6
+
+
+def remote(src, dst, send, recv, device):
+    return pltpu.make_async_remote_copy(
+        src_ref=src,
+        dst_ref=dst,
+        send_sem=send,
+        recv_sem=recv,
+        device_id=device,
+        device_id_type=MESH,
+    )
+
+
+def fused_kernel(rows, cols, slot_ref, block_ref, live_ref, pt_ref, u_ref, pivot_ref, a_ref, *refs):
+    out_ref, diag_ref = refs[:2]
+    gathered = refs[2 : 2 + PARTS]
+    stage = refs[2 + PARTS : 4 + PARTS]
+    (
+        pt, packed, a_high, a_low, m_ref, r1, r2, final, uf, ut_high, ut_low,
+        ph_send, ph_recv, nh_high, nh_low, cit, qp, qc, qb, qd, qz,
+        a_sem, ag_s, ag_r, up_s, up_r, dn_s, dn_r, core_s, core_r, u_s, u_r,
+        ph_s, ph_r, r1_s, r1_r, r2_s, r2_r, out_s, out_r, qc_s, qc_r,
+        qb_s, qb_r, qz_s, qz_r,
+    ) = refs[4 + PARTS :]
+    nz = rows // 2
+    kw, width = u_ref.shape
+    sub = kw // PARTS
+    rows_here, cols_here = a_ref.shape
+    slots = slot_ref.shape[1]
+    chosen = slots * BLK
+    rq = rows_here // cols
+    hq = rq // 2
+    wq = width // cols
+    quarter = rq // BLK
+    tile_rows = rows_here // A_TILES
+
+    r, c = lax.axis_index("row"), lax.axis_index("col")
+    z, p = r // 2, r % 2
+    mate = r + 1 - 2 * p
+    xc = c + 1 - 2 * (c % 2)
+    yc = c + 2 - 4 * (c // 2)
+    dc = 3 - c
+    plane = (xc, yc, dc)
+
+    def a_copy(t):
+        return pltpu.make_async_copy(
+            a_ref.at[pl.ds(t * tile_rows, tile_rows), :], stage[t % 2], a_sem.at[t % 2]
+        )
+
+    a_copy(0).start()
+    a_copy(1).start()
+
+    barrier = pltpu.get_barrier_semaphore()
+    for step in range(1, rows):
+        pl.semaphore_signal(
+            barrier, inc=1, device_id=((r + step) % rows, c), device_id_type=MESH
+        )
+    for other in plane:
+        pl.semaphore_signal(barrier, inc=1, device_id=(r, other), device_id_type=MESH)
+    pl.semaphore_wait(barrier, rows - 1 + cols - 1)
+
+    sent = []
+
+    def start(copy, when=None):
+        sent.append((copy, when))
+        if when is None:
+            copy.start()
+        else:
+            pl.when(when)(copy.start)
+
+    for h in range(PARTS):
+        for i, other in enumerate(plane):
+            start(
+                remote(
+                    pt_ref.at[pl.ds(h * sub, sub), :],
+                    gathered[h].at[c],
+                    ag_s.at[h, i],
+                    ag_r.at[h, i],
+                    (r, other),
+                )
+            )
+    for step in range(1, rows):
+        start(remote(u_ref, uf.at[r], u_s.at[step], u_r.at[step], ((r + step) % rows, c)))
+    uf[r] = u_ref[...]
+    for h in range(PARTS):
+        gathered[h][c] = pt_ref[pl.ds(h * sub, sub), :]
+
+    def prepare(t):
+        a_copy(t).wait()
+        for s in range(slots):
+            column = slot_ref[2, s] * BLK
+            high, low = halves(stage[t % 2][:, pl.ds(column, BLK)])
+            a_high[pl.ds(t * tile_rows, tile_rows), s * BLK : (s + 1) * BLK] = high
+            a_low[pl.ds(t * tile_rows, tile_rows), s * BLK : (s + 1) * BLK] = low
+        if t + 2 < A_TILES:
+            a_copy(t + 2).start()
+
+    def part(h):
+        return pl.ds(h * sub, sub)
+
+    def z_copy(source, h, d, up):
+        send, recv = (up_s, up_r) if up else (dn_s, dn_r)
+        target = r + 2 if up else r - 2
+        where = pt.at[source, part(h), :]
+        return remote(where, where, send.at[d, h], recv.at[d, h], (target, c))
+
+    def core_copy(source, h):
+        where = pt.at[source, part(h), :]
+        return remote(where, where, core_s.at[source // 2, h], core_r.at[source // 2, h], (mate, c))
+
+    def own_part(h):
+        for i, other in enumerate(plane):
+            remote(
+                pt_ref.at[part(h), :], gathered[h].at[other], ag_s.at[h, i], ag_r.at[h, i],
+                (r, other),
+            ).wait_recv()
+        for s in range(slots):
+            offset = slot_ref[1, s] * BLK
+            value = gathered[h][slot_ref[0, s], :, pl.ds(offset, BLK)]
+            pt[r, part(h), s * BLK : (s + 1) * BLK] = value * live_ref[s]
+        start(z_copy(r, h, 0, True), z < nz - 1)
+        start(z_copy(r, h, 0, False), z > 0)
+        start(core_copy(r, h))
+
+    def tick(d, h):
+        for up in (True, False):
+            source = r - 2 * d if up else r + 2 * d
+            there = (source >= 0) & (source < rows)
+            onward = there & ((z < nz - 1) if up else (z > 0))
+            pl.when(there)(lambda: z_copy(source, h, d - 1, up).wait_recv())
+            if d < nz - 1:
+                start(z_copy(source, h, d, up), onward)
+            start(core_copy(source, h), there)
+
+    def chip_at(j):
+        near = jnp.where(z <= nz - 1 - z, z, nz - 1 - z)
+        hop = (j + 1) // 2
+        paired = z + hop if j % 2 else z - hop
+        single = jnp.where(z <= nz - 1 - z, j, nz - 1 - j)
+        return jnp.where(j <= 2 * near, paired, single)
+
+    def pack(j):
+        chip = chip_at(j)
+        for h in range(PARTS):
+            source = 2 * chip + 1 - p
+            where = pt.at[source, part(h), :]
+            remote(where, where, core_s.at[chip, h], core_r.at[chip, h], (mate, c)).wait_recv()
+        for core in range(2):
+            high, low = halves(pt[2 * chip + core])
+            packed[core * kw : (core + 1) * kw, :] = high
+            packed[(2 + core) * kw : (3 + core) * kw, :] = low
+
+    def multiply(j, q, half):
+        at = pl.ds(pl.multiple_of(q * rq + half * hq, 8), hq)
+        both = dot(a_high[at, :], packed[...], NT)
+        cross = dot(a_low[at, :], packed[: 2 * kw, :], NT)
+        m_ref[j, at, :] = both[:, : 2 * kw] + (both[:, 2 * kw :] + cross)
+
+    def tiles(q, half):
+        return pl.ds(pl.multiple_of(q * rq + half * hq, 8), hq)
+
+    first = ((xc, 0, xc, 0), (yc, 1, yc, 0), (dc, 0, xc, 1), (dc, 1, yc, 1))
+    later = ((yc, 0), (xc, 1), (c, 0), (c, 1))
+
+    def r1_copy(j, i):
+        q, half, other, slot = first[i]
+        return remote(
+            m_ref.at[j, tiles(q, half), :],
+            r1.at[j, half, slot],
+            r1_s.at[j, half, slot],
+            r1_r.at[j, half, slot],
+            (r, other),
+        )
+
+    def r2_copy(j, half):
+        return remote(
+            r1.at[j, half, 1], r2.at[j, half], r2_s.at[j, half], r2_r.at[j, half],
+            (r, xc if half else yc),
+        )
+
+    def product_tile(j, i):
+        if i < 4:
+            q, half, _, _ = first[i]
+        else:
+            q, half = later[i - 4]
+        multiply(j, q, half)
+        if i < 4:
+            start(r1_copy(j, i))
+
+    def reduce_first(j):
+        for half in range(2):
+            for i in range(4):
+                if first[i][1] == half and first[i][3] == 1:
+                    r1_copy(j, i).wait_recv()
+            r1[j, half, 1] = r1[j, half, 1] + m_ref[j, tiles(xc if half else yc, half), :]
+            start(r2_copy(j, half))
+
+    def reduce_last(j):
+        lanes = pl.ds(pl.multiple_of(chip_at(j) * 2 * kw, BLK), 2 * kw)
+        for half in range(2):
+            for i in range(4):
+                if first[i][1] == half and first[i][3] == 0:
+                    r1_copy(j, i).wait_recv()
+            r2_copy(j, half).wait_recv()
+            final[half * hq : (half + 1) * hq, lanes] = (
+                m_ref[j, tiles(c, half), :] + r1[j, half, 0] + r2[j, half]
+            )
+
+    def listed_part(h):
+        for target in range(rows):
+            for k in range(quarter):
+                at = target * quarter + k
+                offset = block_ref[1, at] * BLK
+                value = gathered[h][block_ref[0, at], :, pl.ds(offset, BLK)]
+                ph_send[target, part(h), k * BLK : (k + 1) * BLK] = (
+                    value * live_ref[slots + at]
+                )
+
+    def listed_send():
+        for step in range(1, rows):
+            target = (r + step) % rows
+            start(
+                remote(
+                    ph_send.at[target], ph_recv.at[r], ph_s.at[step], ph_r.at[step], (target, c)
+                )
+            )
+        ph_recv[r] = ph_send[r]
+
+    def turn_unit():
+        for step in range(1, rows):
+            source = (r - step + rows) % rows
+            remote(u_ref, uf.at[source], u_s.at[step], u_r.at[step], (r, c)).wait_recv()
+        for chip in range(nz):
+            both = jnp.concatenate([uf[2 * chip], uf[2 * chip + 1]], axis=0)
+            high, low = halves(both.T)
+            ut_high[:, chip * 2 * kw : (chip + 1) * 2 * kw] = high
+            ut_low[:, chip * 2 * kw : (chip + 1) * 2 * kw] = low
+
+    def normalise_listed():
+        for step in range(1, rows):
+            source = (r - step + rows) % rows
+            remote(
+                ph_send.at[source], ph_recv.at[source], ph_s.at[step], ph_r.at[step], (r, c)
+            ).wait_recv()
+        value = halves(ph_recv[...].reshape(width, rq))
+        high, low = halves(dot3((ut_high[...], ut_low[...]), value, NN))
+        nh_high[...] = high
+        nh_low[...] = low
+
+    for t in range(A_TILES - 2):
+        prepare(t)
+    for h in range(PARTS):
+        own_part(h)
+        if h < 2:
+            prepare(A_TILES - 2 + h)
+
+    for j in range(nz):
+        pack(j)
+        for h in range(PARTS):
+            product_tile(j, 2 * h)
+            product_tile(j, 2 * h + 1)
+            if j + 1 < nz:
+                tick(j + 1, h)
+            if j == 0:
+                listed_part(h)
+            if h == 1 and j >= 1:
+                reduce_first(j - 1)
+        if j >= 2:
+            reduce_last(j - 2)
+        if j == 1:
+            listed_send()
+            turn_unit()
+        if j == 2:
+            normalise_listed()
+    reduce_first(nz - 1)
+    reduce_last(nz - 2)
+    reduce_last(nz - 1)
+
+    f_halves = halves(final[...])
+    result = -dot3((ut_high[...], ut_low[...]), f_halves, NT)
+    cit[...] = result
+
+    def out_copy(i, other, source):
+        return remote(
+            cit.at[pl.ds(pl.multiple_of(other * wq, 8), wq), :],
+            out_ref.at[:, pl.ds(pl.multiple_of(source * rq, BLK), rq)],
+            out_s.at[i],
+            out_r.at[i],
+            (r, other),
+        )
+
+    for i, other in enumerate(plane):
+        start(out_copy(i, other, c))
+
+    ci = halves(result)
+    for chip in range(nz):
+        at = slice(chip * 2 * kw, (chip + 1) * 2 * kw)
+        value = dot3((nh_high[at, :], nh_low[at, :]), ci, NT)
+        qp[0, chip] = value[:kw]
+        qp[1, chip] = value[kw:]
+    core_sum = remote(qp.at[1 - p], qc, qc_s, qc_r, (mate, c))
+    start(core_sum)
+    out_ref[:, pl.ds(pl.multiple_of(c * rq, BLK), rq)] = cit[pl.ds(pl.multiple_of(c * wq, 8), wq), :]
+    core_sum.wait_recv()
+    qc[...] = qc[...] + qp[p]
+
+    def lanes_of(column):
+        return pl.ds(pl.multiple_of(column * wq, BLK), wq)
+
+    def plane_copy(i, other):
+        return remote(qc.at[:, :, lanes_of(other)], qb.at[i], qb_s.at[i], qb_r.at[i], (r, other))
+
+    for i, other in enumerate(plane):
+        start(plane_copy(i, other))
+    for i, other in enumerate(plane):
+        plane_copy(i, other).wait_recv()
+    qd[...] = qc[:, :, lanes_of(c)] + (qb[0] + (qb[1] + qb[2]))
+    for step in range(1, nz):
+        target = (z + step) % nz
+        start(
+            remote(
+                qd.at[target], qz.at[step], qz_s.at[step], qz_r.at[step], (2 * target + p, c)
+            )
+        )
+    for step in range(1, nz):
+        remote(qd.at[step], qz.at[step], qz_s.at[step], qz_r.at[step], (r, c)).wait_recv()
+    total = qd[z]
+    for step in range(1, nz):
+        total = total + qz[step]
+    diag_ref[...] = pivot_ref[...] - total
+
+    for i, other in enumerate(plane):
+        out_copy(i, other, other).wait_recv()
+    for copy, when in sent:
+        if when is None:
+            copy.wait_send()
+        else:
+            pl.when(when)(copy.wait_send)
+
+
+def fused(rows, cols, ancestor_inverse, panel, unit_inverse, pivot_inverse, panel_blocks):
+    rows_here, cols_here = ancestor_inverse.shape
+    stored, kw = panel.shape
+    width = unit_inverse.shape[1]
+    row_blocks, range_blocks = rows_here // BLK, cols_here // BLK
+    slot_ids, block_ids, live = tables(panel_blocks, cols, range_blocks, row_blocks, rows)
+    slots = range_blocks // 2
+    chosen = slots * BLK
+    nz = rows // 2
+    rq, wq = rows_here // cols, width // cols
+    f32, bf16 = jnp.float32, jnp.bfloat16
+    dma = pltpu.SemaphoreType.DMA
+    vmem = pl.BlockSpec(memory_space=pltpu.VMEM)
+    smem = pl.BlockSpec(memory_space=pltpu.SMEM)
+    scratch = (
+        [pltpu.VMEM((cols, kw // PARTS, stored), f32)] * PARTS
+        + [pltpu.VMEM((rows_here // A_TILES, cols_here), f32)] * 2
+        + [
+            pltpu.VMEM((rows, kw, chosen), f32),
+            pltpu.VMEM((4 * kw, chosen), bf16),
+            pltpu.VMEM((rows_here, chosen), bf16),
+            pltpu.VMEM((rows_here, chosen), bf16),
+            pltpu.VMEM((nz, rows_here, 2 * kw), f32),
+            pltpu.VMEM((nz, 2, 2, rq // 2, 2 * kw), f32),
+            pltpu.VMEM((nz, 2, rq // 2, 2 * kw), f32),
+            pltpu.VMEM((rq, width), f32),
+            pltpu.VMEM((rows, kw, width), f32),
+            pltpu.VMEM((width, width), bf16),
+            pltpu.VMEM((width, width), bf16),
+            pltpu.VMEM((rows, kw, rq), f32),
+            pltpu.VMEM((rows, kw, rq), f32),
+            pltpu.VMEM((width, rq), bf16),
+            pltpu.VMEM((width, rq), bf16),
+            pltpu.VMEM((width, rq), f32),
+            pltpu.VMEM((2, nz, kw, width), f32),
+            pltpu.VMEM((nz, kw, width), f32),
+            pltpu.VMEM((cols - 1, nz, kw, wq), f32),
+            pltpu.VMEM((nz, kw, wq), f32),
+            pltpu.VMEM((nz, kw, wq), f32),
+            dma((2,)),
+            dma((PARTS, cols - 1)),
+            dma((PARTS, cols - 1)),
+            dma((nz, PARTS)),
+            dma((nz, PARTS)),
+            dma((nz, PARTS)),
+            dma((nz, PARTS)),
+            dma((nz, PARTS)),
+            dma((nz, PARTS)),
+            dma((rows,)),
+            dma((rows,)),
+            dma((rows,)),
+            dma((rows,)),
+            dma((nz, 2, 2)),
+            dma((nz, 2, 2)),
+            dma((nz, 2)),
+            dma((nz, 2)),
+            dma((cols - 1,)),
+            dma((cols - 1,)),
+            dma,
+            dma,
+            dma((cols - 1,)),
+            dma((cols - 1,)),
+            dma((nz,)),
+            dma((nz,)),
+        ]
+    )
+    return pl.pallas_call(
+        functools.partial(fused_kernel, rows, cols),
+        out_shape=(
+            jax.ShapeDtypeStruct((wq, rows_here), f32),
+            jax.ShapeDtypeStruct(pivot_inverse.shape, f32),
+        ),
+        in_specs=[smem, smem, smem, vmem, vmem, vmem, pl.BlockSpec(memory_space=pl.ANY)],
+        out_specs=(vmem, vmem),
+        scratch_shapes=scratch,
+        compiler_params=pltpu.CompilerParams(
+            collective_id=0, has_side_effects=True, vmem_limit_bytes=62 << 20
+        ),
+    )(slot_ids, block_ids, live, panel.T, unit_inverse, pivot_inverse, ancestor_inverse)
+
+
+def fits(mesh, ancestor_inverse, panel, unit_inverse):
+    rows, cols = mesh.shape["row"], mesh.shape["col"]
+    rows_here = ancestor_inverse.shape[0] // rows
+    width = unit_inverse.shape[1]
+    return (
+        cols == 4
+        and rows % 2 == 0
+        and rows_here % (cols * BLK) == 0
+        and rows_here % (16 * A_TILES) == 0
+        and width == BLK * (rows // 2)
+        and panel.shape[0] % (cols * BLK) == 0
+        and ancestor_inverse.shape[1] % (2 * cols * BLK) == 0
+    )
+
+
 def solution(mesh):
-    return jax.shard_map(
-        on_device,
-        mesh=mesh,
-        in_specs=(P("row", "col"), P("col", "row"), P("row", None), P("row", "col"), P()),
-        out_specs=(P("col", "row"), P("row", "col")),
-        check_vma=False,
-    )
+    rows, cols = mesh.shape["row"], mesh.shape["col"]
+
+    def whole(ancestor_inverse, panel, unit_inverse, pivot_inverse, panel_blocks):
+        body = on_device
+        if fits(mesh, ancestor_inverse, panel, unit_inverse):
+            body = functools.partial(fused, rows, cols)
+        return jax.shard_map(
+            body,
+            mesh=mesh,
+            in_specs=(P("row", "col"), P("col", "row"), P("row", None), P("row", "col"), P()),
+            out_specs=(P("col", "row"), P("row", "col")),
+            check_vma=False,
+        )(ancestor_inverse, panel, unit_inverse, pivot_inverse, panel_blocks)
+
+    return whole

time: 218 us -> 110 us (0.50)
  blocking collectives: 92 us -> 0 us
  Pallas kernels: 23.7 us -> 105 us
  waiting for transfers between devices: 68.8 us -> 0 us
  between operations: 13.9 us -> 0.65 us
  matrix products: 12.2 us -> 0 us
  other arithmetic: 3.35 us -> 0 us
    pallas_call x3 -> x2, Pallas kernels: 23.7 us -> 105 us  [the longest x1 102 us: fused(): pl.pallas_call(functools.partial(fused_kernel, rows, cols), out_shape=(ja...]
    all_to_all x2 -> x0, blocking collectives: 60.7 us -> none  [the longest x1 46.6 us: on_device(): lax.all_to_all(select(share, block_ids, block_live, rows), 'row', 0, 0)]
    reduce_scatter x1 -> x0, waiting for transfers between devices: 42.4 us -> none  [on_device(): lax.psum_scatter(product(normal, ancestor_inverse, local_ids), 'col', sca...]
    all_gather x2 -> x0, blocking collectives: 31.3 us -> none  [on_device(): lax.all_gather(unit_inverse[:, k * half:(k + 1) * half], 'row', axis=0, t...]
    all_gather x3 -> x0, waiting for transfers between devices: 25.7 us -> none  [the longest x1 21 us: on_device(): lax.all_gather(listed, 'col', axis=0, tiled=False).reshape(width, rows_here)]
    dot_general x3 -> x0, matrix products: 12.2 us -> none  [the longest x2 9.67 us: normalise(): lax.dot_general(factor, value, (((0,), (0,)), ((), ())), precision=high,...]
    unnamed x7 -> x2, local copies, waits for them, and re-layouts: 0.07 us -> 3.44 us
  transfers between devices with their start and end apart: 4 -> 0, of which waited for: 4 -> 0; matrix products, arithmetic and copies ran while one was open for 7% -> 0% of each run, Pallas kernels for 10% -> 0%
where the time goes in v1:
time: 110 us; the launch traced here: 109 us
  Pallas kernels  105 us (95%)
  local copies, waits for them, and re-layouts  3.44 us (3%)
    pallas_call x1, Pallas kernels, fused(): pl.pallas_call(functools.partial(fused_kernel, rows, cols), out_shape=(ja...  102 us
    unnamed x2, local copies, waits for them, and re-layouts  3.44 us
    pallas_call x1, Pallas kernels, tables(): pl.pallas_call(functools.partial(table_kernel, cols, range_blocks, row_bl...  2.87 us

profile of v1, /device:TPU:0, one launch (start us, length us, event | category | flops | bytes accessed | tf_op | source)
XLA Modules:
  0.0 109.3 jit_solution(11559907088501334252)
XLA Ops:
  0.6 2.9 %shard_map.68 = (s32[3,12]{1,0:T(4,128)}, s32[2,24]{1,0:T(2,128)}, f32[36]{0:T(128)}) custom-call(s32[44]{0:T(128)} %ids_ref.1), custom_call_target="tpu_custom_call" | custom-call | tf_op jit(solution)/shard_map/pallas_call | solution.py:208
  3.5 102.4 %shard_map.69 = (f32[128,1536]{1,0:T(8,128)}, f32[64,128]{1,0:T(8,128)}) custom-call(s32[3,12]{1,0:T(4,128)} %get-tuple-element.5.slot_ref, s32[2,24]{1,0:T(2,128)} %get-tuple-element.6.block_ref, f32[36]{0:T(128)} %get-tuple-element.7.live_ref, f32[64,1408]{1,0:T(8,128)} %bitcast.1, f32[64,512]{1,0:T(8,128)} %u_ref.1, f32[64,128]{1,0:T(8,128)} %pivot_ref.1, ...), custom_call_target="tpu_custom_call" | custom-call | tf_op jit(solution)/shard_map/pallas_call | solution.py:640
  105.9 2.1 %copy.9 = f32[128,1536]{1,0:T(8,128)} copy(f32[128,1536]{1,0:T(8,128)} %get-tuple-element.10) | data formatting | bytes 1572864
  108.0 1.4 %copy.10 = f32[64,128]{1,0:T(8,128)} copy(f32[64,128]{1,0:T(8,128)} %get-tuple-element.11) | data formatting | bytes 65536

commit v2 on v1

--- a/solution.py
+++ b/solution.py
@@ -251,7 +251,7 @@
     (
         pt, packed, a_high, a_low, m_ref, r1, r2, final, uf, ut_high, ut_low,
         ph_send, ph_recv, nh_high, nh_low, cit, qp, qc, qb, qd, qz,
-        a_sem, ag_s, ag_r, up_s, up_r, dn_s, dn_r, core_s, core_r, u_s, u_r,
+        a_sem, ag_s, ag_r, up_s, up_r, dn_s, dn_r, core_s, core_r, uu_s, uu_r, ud_s, ud_r, um_s, um_r,
         ph_s, ph_r, r1_s, r1_r, r2_s, r2_r, out_s, out_r, qc_s, qc_r,
         qb_s, qb_r, qz_s, qz_r,
     ) = refs[4 + PARTS :]
@@ -301,22 +301,58 @@
         else:
             pl.when(when)(copy.start)
 
+    def part(h):
+        return pl.ds(h * sub, sub)
+
+    def own_copy(h, i, source):
+        return remote(
+            pt_ref.at[part(h), :],
+            gathered[h].at[source],
+            ag_s.at[h, i],
+            ag_r.at[h, i],
+            (r, plane[i]),
+        )
+
+    def own_send(h):
+        for i in range(cols - 1):
+            start(own_copy(h, i, c))
+
+    own_send(0)
+    def unit_copy(source, chip, d, up):
+        send, recv = (uu_s, uu_r) if up else (ud_s, ud_r)
+        where = uf.at[source, :, pl.ds(0, 2 * kw * (chip + 1))]
+        data = u_ref.at[:, pl.ds(0, 2 * kw * (chip + 1))] if d == 0 else where
+        return remote(data, where, send.at[d], recv.at[d], (r + 2 if up else r - 2, c))
+
+    def unit_mate(source):
+        where = uf.at[source]
+        return remote(where, where, um_s.at[source // 2], um_r.at[source // 2], (mate, c))
+
+    for chip in range(nz):
+        if chip < nz - 1:
+            start(unit_copy(r, chip, 0, True), z == chip)
+        if chip > 0:
+            start(unit_copy(r, chip, 0, False), z == chip)
+    for chip in range(nz - 1):
+        uf[2 * chip + p, :, 2 * kw * (chip + 1) :] = jnp.zeros(
+            (kw, width - 2 * kw * (chip + 1)), jnp.float32
+        )
+    own_unit = remote(u_ref, uf.at[r], um_s.at[z], um_r.at[z], (mate, c))
+    start(own_unit)
+
+    def unit_tick(d):
+        for up in (True, False):
+            source = r - 2 * d if up else r + 2 * d
+            for chip in range(nz):
+                at = z - d == chip if up else z + d == chip
+                onward = at & ((z < nz - 1) if up else (z > 0))
+                pl.when(at)(unit_copy(source, chip, d - 1, up).wait_recv)
+                if d < nz - 1:
+                    start(unit_copy(source, chip, d, up), onward)
+            start(unit_mate(source), (source >= 0) & (source < rows))
+
     for h in range(PARTS):
-        for i, other in enumerate(plane):
-            start(
-                remote(
-                    pt_ref.at[pl.ds(h * sub, sub), :],
-                    gathered[h].at[c],
-                    ag_s.at[h, i],
-                    ag_r.at[h, i],
-                    (r, other),
-                )
-            )
-    for step in range(1, rows):
-        start(remote(u_ref, uf.at[r], u_s.at[step], u_r.at[step], ((r + step) % rows, c)))
-    uf[r] = u_ref[...]
-    for h in range(PARTS):
-        gathered[h][c] = pt_ref[pl.ds(h * sub, sub), :]
+        gathered[h][c] = pt_ref[part(h), :]
 
     def prepare(t):
         a_copy(t).wait()
@@ -328,9 +364,6 @@
         if t + 2 < A_TILES:
             a_copy(t + 2).start()
 
-    def part(h):
-        return pl.ds(h * sub, sub)
-
     def z_copy(source, h, d, up):
         send, recv = (up_s, up_r) if up else (dn_s, dn_r)
         target = r + 2 if up else r - 2
@@ -342,11 +375,8 @@
         return remote(where, where, core_s.at[source // 2, h], core_r.at[source // 2, h], (mate, c))
 
     def own_part(h):
-        for i, other in enumerate(plane):
-            remote(
-                pt_ref.at[part(h), :], gathered[h].at[other], ag_s.at[h, i], ag_r.at[h, i],
-                (r, other),
-            ).wait_recv()
+        for i in range(cols - 1):
+            own_copy(h, i, plane[i]).wait_recv()
         for s in range(slots):
             offset = slot_ref[1, s] * BLK
             value = gathered[h][slot_ref[0, s], :, pl.ds(offset, BLK)]
@@ -460,9 +490,9 @@
         ph_recv[r] = ph_send[r]
 
     def turn_unit():
-        for step in range(1, rows):
-            source = (r - step + rows) % rows
-            remote(u_ref, uf.at[source], u_s.at[step], u_r.at[step], (r, c)).wait_recv()
+        uf[r] = u_ref[...]
+        for chip in range(nz):
+            unit_mate(2 * chip + 1 - p).wait_recv()
         for chip in range(nz):
             both = jnp.concatenate([uf[2 * chip], uf[2 * chip + 1]], axis=0)
             high, low = halves(both.T)
@@ -480,39 +510,6 @@
         nh_high[...] = high
         nh_low[...] = low
 
-    for t in range(A_TILES - 2):
-        prepare(t)
-    for h in range(PARTS):
-        own_part(h)
-        if h < 2:
-            prepare(A_TILES - 2 + h)
-
-    for j in range(nz):
-        pack(j)
-        for h in range(PARTS):
-            product_tile(j, 2 * h)
-            product_tile(j, 2 * h + 1)
-            if j + 1 < nz:
-                tick(j + 1, h)
-            if j == 0:
-                listed_part(h)
-            if h == 1 and j >= 1:
-                reduce_first(j - 1)
-        if j >= 2:
-            reduce_last(j - 2)
-        if j == 1:
-            listed_send()
-            turn_unit()
-        if j == 2:
-            normalise_listed()
-    reduce_first(nz - 1)
-    reduce_last(nz - 2)
-    reduce_last(nz - 1)
-
-    f_halves = halves(final[...])
-    result = -dot3((ut_high[...], ut_low[...]), f_halves, NT)
-    cit[...] = result
-
     def out_copy(i, other, source):
         return remote(
             cit.at[pl.ds(pl.multiple_of(other * wq, 8), wq), :],
@@ -522,20 +519,24 @@
             (r, other),
         )
 
-    for i, other in enumerate(plane):
-        start(out_copy(i, other, c))
-
-    ci = halves(result)
-    for chip in range(nz):
-        at = slice(chip * 2 * kw, (chip + 1) * 2 * kw)
-        value = dot3((nh_high[at, :], nh_low[at, :]), ci, NT)
-        qp[0, chip] = value[:kw]
-        qp[1, chip] = value[kw:]
+    def unit_product():
+        cit[...] = -dot3((ut_high[...], ut_low[...]), halves(final[...]), NT)
+        for i, other in enumerate(plane):
+            start(out_copy(i, other, c))
+        out_ref[:, pl.ds(pl.multiple_of(c * rq, BLK), rq)] = cit[
+            pl.ds(pl.multiple_of(c * wq, 8), wq), :
+        ]
+
     core_sum = remote(qp.at[1 - p], qc, qc_s, qc_r, (mate, c))
-    start(core_sum)
-    out_ref[:, pl.ds(pl.multiple_of(c * rq, BLK), rq)] = cit[pl.ds(pl.multiple_of(c * wq, 8), wq), :]
-    core_sum.wait_recv()
-    qc[...] = qc[...] + qp[p]
+
+    def listed_product():
+        ci = halves(cit[...])
+        for chip in range(nz):
+            at = slice(chip * 2 * kw, (chip + 1) * 2 * kw)
+            value = dot3((nh_high[at, :], nh_low[at, :]), ci, NT)
+            qp[0, chip] = value[:kw]
+            qp[1, chip] = value[kw:]
+        start(core_sum)
 
     def lanes_of(column):
         return pl.ds(pl.multiple_of(column * wq, BLK), wq)
@@ -543,32 +544,93 @@
     def plane_copy(i, other):
         return remote(qc.at[:, :, lanes_of(other)], qb.at[i], qb_s.at[i], qb_r.at[i], (r, other))
 
-    for i, other in enumerate(plane):
-        start(plane_copy(i, other))
-    for i, other in enumerate(plane):
-        plane_copy(i, other).wait_recv()
-    qd[...] = qc[:, :, lanes_of(c)] + (qb[0] + (qb[1] + qb[2]))
-    for step in range(1, nz):
-        target = (z + step) % nz
-        start(
-            remote(
-                qd.at[target], qz.at[step], qz_s.at[step], qz_r.at[step], (2 * target + p, c)
+    def sum_cores():
+        core_sum.wait_recv()
+        qc[...] = qc[...] + qp[p]
+        for i, other in enumerate(plane):
+            start(plane_copy(i, other))
+
+    def sum_plane():
+        for i, other in enumerate(plane):
+            plane_copy(i, other).wait_recv()
+        qd[...] = qc[:, :, lanes_of(c)] + (qb[0] + (qb[1] + qb[2]))
+        for step in range(1, nz):
+            target = (z + step) % nz
+            start(
+                remote(
+                    qd.at[target], qz.at[step], qz_s.at[step], qz_r.at[step], (2 * target + p, c)
+                )
             )
-        )
-    for step in range(1, nz):
-        remote(qd.at[step], qz.at[step], qz_s.at[step], qz_r.at[step], (r, c)).wait_recv()
-    total = qd[z]
-    for step in range(1, nz):
-        total = total + qz[step]
-    diag_ref[...] = pivot_ref[...] - total
-
-    for i, other in enumerate(plane):
-        out_copy(i, other, other).wait_recv()
-    for copy, when in sent:
-        if when is None:
-            copy.wait_send()
-        else:
-            pl.when(when)(copy.wait_send)
+
+    def sum_line():
+        for step in range(1, nz):
+            remote(qd.at[step], qz.at[step], qz_s.at[step], qz_r.at[step], (r, c)).wait_recv()
+        total = qd[z]
+        for step in range(1, nz):
+            total = total + qz[step]
+        diag_ref[...] = pivot_ref[...] - total
+
+    def finish():
+        for i, other in enumerate(plane):
+            out_copy(i, other, other).wait_recv()
+        for copy, when in sent:
+            if when is None:
+                copy.wait_send()
+            else:
+                pl.when(when)(copy.wait_send)
+
+    prepare(0)
+    prepare(1)
+    prepare(2)
+    prepare(3)
+    own_send(1)
+    unit_tick(1)
+    prepare(4)
+    own_part(0)
+    own_send(2)
+    unit_tick(2)
+    prepare(5)
+    own_part(1)
+    own_send(3)
+    tick(1, 0)
+    own_part(2)
+    tick(1, 1)
+    own_part(3)
+    tick(2, 0)
+    unit_tick(3)
+    tick(1, 2)
+
+    between = {
+        (0, 1): (2, 1), (0, 3): (1, 3), (0, 7): (2, 2), (1, 1): (2, 3), (1, 4): (3, 0),
+        (1, 7): (3, 1), (2, 2): (3, 2), (2, 5): (3, 3),
+    }
+    for j in range(nz):
+        pack(j)
+        for i in range(8):
+            product_tile(j, i)
+            if (j, i) in between:
+                tick(*between[j, i])
+            if j == 0 and i == 4:
+                for h in range(PARTS):
+                    listed_part(h)
+            if j == 1 and i == 4:
+                turn_unit()
+            if j >= 1 and i == 4:
+                reduce_first(j - 1)
+            if j >= 2 and i == 6:
+                reduce_last(j - 2)
+        if j == nz - 2:
+            listed_send()
+    reduce_first(nz - 1)
+    reduce_last(nz - 2)
+    reduce_last(nz - 1)
+    unit_product()
+    normalise_listed()
+    listed_product()
+    sum_cores()
+    sum_plane()
+    sum_line()
+    finish()
 
 
 def fused(rows, cols, ancestor_inverse, panel, unit_inverse, pivot_inverse, panel_blocks):
@@ -619,8 +681,12 @@
             dma((nz, PARTS)),
             dma((nz, PARTS)),
             dma((nz, PARTS)),
-            dma((rows,)),
-            dma((rows,)),
+            dma((nz,)),
+            dma((nz,)),
+            dma((nz,)),
+            dma((nz,)),
+            dma((nz,)),
+            dma((nz,)),
             dma((rows,)),
             dma((rows,)),
             dma((nz, 2, 2)),

time: 110 us -> 90.3 us (0.82)
  Pallas kernels: 105 us -> 86 us
    pallas_call x1, Pallas kernels: 102 us -> 83.1 us  [fused(): pl.pallas_call(functools.partial(fused_kernel, rows, cols), out_shape=(ja...]
where the time goes in v2:
time: 90.3 us; the launch traced here: 90.1 us
  Pallas kernels  86 us (95%)
  local copies, waits for them, and re-layouts  3.44 us (4%)
    pallas_call x1, Pallas kernels, fused(): pl.pallas_call(functools.partial(fused_kernel, rows, cols), out_shape=(ja...  83.1 us
    unnamed x2, local copies, waits for them, and re-layouts  3.44 us
    pallas_call x1, Pallas kernels, tables(): pl.pallas_call(functools.partial(table_kernel, cols, range_blocks, row_bl...  2.87 us

profile of v2, /device:TPU:0, one launch (start us, length us, event | category | flops | bytes accessed | tf_op | source)
XLA Modules:
  0.0 90.1 jit_solution(14637535319685081988)
XLA Ops:
  0.6 2.9 %shard_map.68 = (s32[3,12]{1,0:T(4,128)}, s32[2,24]{1,0:T(2,128)}, f32[36]{0:T(128)}) custom-call(s32[44]{0:T(128)} %ids_ref.1), custom_call_target="tpu_custom_call" | custom-call | tf_op jit(solution)/shard_map/pallas_call | solution.py:208
  3.5 83.1 %shard_map.69 = (f32[128,1536]{1,0:T(8,128)}, f32[64,128]{1,0:T(8,128)}) custom-call(s32[3,12]{1,0:T(4,128)} %get-tuple-element.5.slot_ref, s32[2,24]{1,0:T(2,128)} %get-tuple-element.6.block_ref, f32[36]{0:T(128)} %get-tuple-element.7.live_ref, f32[64,1408]{1,0:T(8,128)} %bitcast.1, f32[64,512]{1,0:T(8,128)} %u_ref.1, f32[64,128]{1,0:T(8,128)} %pivot_ref.1, ...), custom_call_target="tpu_custom_call" | custom-call | tf_op jit(solution)/shard_map/pallas_call | solution.py:706
  86.6 2.1 %copy.9 = f32[128,1536]{1,0:T(8,128)} copy(f32[128,1536]{1,0:T(8,128)} %get-tuple-element.10) | data formatting | bytes 1572864
  88.7 1.4 %copy.10 = f32[64,128]{1,0:T(8,128)} copy(f32[64,128]{1,0:T(8,128)} %get-tuple-element.11) | data formatting | bytes 65536

commit v3 on v2

--- a/solution.py
+++ b/solution.py
@@ -601,11 +601,13 @@
     tick(1, 2)
 
     between = {
-        (0, 1): (2, 1), (0, 3): (1, 3), (0, 7): (2, 2), (1, 1): (2, 3), (1, 4): (3, 0),
-        (1, 7): (3, 1), (2, 2): (3, 2), (2, 5): (3, 3),
+        (0, 1): (2, 1), (0, 3): (1, 3), (0, 7): (2, 2), (1, 7): (2, 3), (2, 1): (3, 0),
+        (2, 3): (3, 1), (2, 5): (3, 2), (2, 7): (3, 3),
     }
     for j in range(nz):
         pack(j)
+        if j == nz - 1:
+            listed_send()
         for i in range(8):
             product_tile(j, i)
             if (j, i) in between:
@@ -619,8 +621,6 @@
                 reduce_first(j - 1)
             if j >= 2 and i == 6:
                 reduce_last(j - 2)
-        if j == nz - 2:
-            listed_send()
     reduce_first(nz - 1)
     reduce_last(nz - 2)
     reduce_last(nz - 1)
@@ -713,7 +713,7 @@
         out_specs=(vmem, vmem),
         scratch_shapes=scratch,
         compiler_params=pltpu.CompilerParams(
-            collective_id=0, has_side_effects=True, vmem_limit_bytes=62 << 20
+            collective_id=0, has_side_effects=True, vmem_limit_bytes=50 << 20
         ),
     )(slot_ids, block_ids, live, panel.T, unit_inverse, pivot_inverse, ancestor_inverse)
 

time: 90.3 us -> 90.6 us (level)
  local copies, waits for them, and re-layouts: 3.44 us -> 6.09 us
  Pallas kernels: 86 us -> 83.6 us
    unnamed x2 -> x14, local copies, waits for them, and re-layouts: 3.44 us -> 6.09 us
    pallas_call x1, Pallas kernels: 83.1 us -> 80.7 us  [fused(): pl.pallas_call(functools.partial(fused_kernel, rows, cols), out_shape=(ja...]
where the time goes in v3:
time: 90.6 us; the launch traced here: 90.3 us
  Pallas kernels  83.6 us (92%)
  local copies, waits for them, and re-layouts  6.09 us (7%)
    pallas_call x1, Pallas kernels, fused(): pl.pallas_call(functools.partial(fused_kernel, rows, cols), out_shape=(ja...  80.7 us
    unnamed x14, local copies, waits for them, and re-layouts  6.09 us
    pallas_call x1, Pallas kernels, tables(): pl.pallas_call(functools.partial(table_kernel, cols, range_blocks, row_bl...  2.87 us

profile of v3, /device:TPU:0, one launch (start us, length us, event | category | flops | bytes accessed | tf_op | source)
XLA Modules:
  0.0 90.3 jit_solution(10624959937516043152)
XLA Ops:
  0.6 2.9 %shard_map.68 = (s32[3,12]{1,0:T(4,128)}, s32[2,24]{1,0:T(2,128)}, f32[36]{0:T(128)}) custom-call(s32[44]{0:T(128)} %ids_ref.1), custom_call_target="tpu_custom_call" | custom-call | tf_op jit(solution)/shard_map/pallas_call | solution.py:208
  3.5 0.0 copy-start
  3.5 1.0 %copy-done = f32[1408,64]{0,1:T(8,128)S(1)} copy-done((f32[1408,64]{0,1:T(8,128)S(1)}, f32[1408,64]{0,1:T(8,128)}, u32[]{:S(2)}) %copy-start) | copy-done | bytes 360472
  4.5 0.0 copy-start.1
  4.5 0.9 copy-done.1
  5.4 0.0 copy-start.2
  5.4 0.8 copy-done.2
  6.2 0.0 copy-start.3
  6.2 0.7 copy-done.3
  6.8 0.0 copy-start.4
  6.8 0.7 copy-done.4
  7.5 0.0 copy-start.5
  7.5 0.6 copy-done.5
  8.1 80.7 %shard_map.69 = (f32[128,1536]{1,0:T(8,128)S(1)}, f32[64,128]{1,0:T(8,128)S(1)}) custom-call(s32[3,12]{1,0:T(4,128)S(1)} %copy-done.3, s32[2,24]{1,0:T(2,128)S(1)} %copy-done.4, f32[36]{0:T(128)S(1)} %copy-done.5, f32[64,1408]{1,0:T(8,128)S(1)} %bitcast.1, f32[64,512]{1,0:T(8,128)S(1)} %copy-done.1, f32[64,128]{1,0:T(8,128)S(1)} %copy-done.2, f32[1536,3072]{1,0:T(8,128)} %a_ref.1), custom_call_target="tpu_custom_call" | custom-call | tf_op jit(solution)/shard_map/pallas_call | solution.py:706
  88.8 0.9 copy.9
  89.7 0.6 copy.10
Async XLA Ops:
  3.5 1.0 %copy-start = (f32[1408,64]{0,1:T(8,128)S(1)}, f32[1408,64]{0,1:T(8,128)}, u32[]{:S(2)}) copy-start(f32[1408,64]{0,1:T(8,128)} %param.6) | copy-start | bytes 1081348
  4.5 0.9 %copy-start.1 = (f32[64,512]{1,0:T(8,128)S(1)}, f32[64,512]{1,0:T(8,128)}, u32[]{:S(2)}) copy-start(f32[64,512]{1,0:T(8,128)} %u_ref.1) | copy-start | bytes 393220
  5.4 0.8 copy-start.2
  6.2 0.7 copy-start.3
  6.8 0.7 copy-start.4
  7.5 0.6 copy-start.5

commit v4 on v3

--- a/solution.py
+++ b/solution.py
@@ -160,18 +160,12 @@
     return (inverse_tile, diagonal_block)
 
 
-def table_kernel(cols, range_blocks, row_blocks, per_shard, ids_ref, slot_ref, block_ref, live_ref):
+def table_kernel(cols, range_blocks, row_blocks, per_shard, ids_ref, table_ref):
     c = lax.axis_index("col")
-    slots = slot_ref.shape[1]
+    slots = range_blocks // 2
     quarter = row_blocks // cols
-    for at in range(slots):
-        for field in range(3):
-            slot_ref[field, at] = 0
-    for at in range(block_ref.shape[1]):
-        for field in range(2):
-            block_ref[field, at] = 0
-    for at in range(live_ref.shape[0]):
-        live_ref[at] = 0.0
+    for at in range(table_ref.shape[0]):
+        table_ref[at] = 0
 
     def step(k, rank):
         block = ids_ref[k]
@@ -182,10 +176,10 @@
 
         @pl.when(here)
         def _():
-            slot_ref[0, rank] = shard
-            slot_ref[1, rank] = offset
-            slot_ref[2, rank] = local
-            live_ref[rank] = 1.0
+            table_ref[rank] = shard
+            table_ref[slots + rank] = offset
+            table_ref[2 * slots + rank] = local
+            table_ref[3 * slots + rank] = 1
 
         row = block // row_blocks
         within = block % row_blocks
@@ -193,9 +187,9 @@
         @pl.when(within // quarter == c)
         def _():
             at = row * quarter + within % quarter
-            block_ref[0, at] = shard
-            block_ref[1, at] = offset
-            live_ref[slots + at] = 1.0
+            table_ref[4 * slots + 3 * at] = shard
+            table_ref[4 * slots + 3 * at + 1] = offset
+            table_ref[4 * slots + 3 * at + 2] = 1
 
         return rank + here.astype(jnp.int32)
 
@@ -209,13 +203,9 @@
         functools.partial(
             table_kernel, cols, range_blocks, row_blocks, ids.shape[0] // cols
         ),
-        out_shape=(
-            jax.ShapeDtypeStruct((3, range_blocks // 2), jnp.int32),
-            jax.ShapeDtypeStruct((2, rows * quarter), jnp.int32),
-            jax.ShapeDtypeStruct((range_blocks // 2 + rows * quarter,), jnp.float32),
-        ),
+        out_shape=jax.ShapeDtypeStruct((2 * range_blocks + 3 * rows * quarter,), jnp.int32),
         in_specs=[smem],
-        out_specs=(smem, smem, smem),
+        out_specs=smem,
     )(ids)
 
 
@@ -244,14 +234,14 @@
     )
 
 
-def fused_kernel(rows, cols, slot_ref, block_ref, live_ref, pt_ref, u_ref, pivot_ref, a_ref, *refs):
+def fused_kernel(rows, cols, table_ref, pt_ref, u_ref, pivot_hbm, a_ref, *refs):
     out_ref, diag_ref = refs[:2]
     gathered = refs[2 : 2 + PARTS]
     stage = refs[2 + PARTS : 4 + PARTS]
     (
         pt, packed, a_high, a_low, m_ref, r1, r2, final, uf, ut_high, ut_low,
         ph_send, ph_recv, nh_high, nh_low, cit, qp, qc, qb, qd, qz,
-        a_sem, ag_s, ag_r, up_s, up_r, dn_s, dn_r, core_s, core_r, uu_s, uu_r, ud_s, ud_r, um_s, um_r,
+        unit_own, pivot_ref, in_sem, a_sem, ag_s, ag_r, up_s, up_r, dn_s, dn_r, core_s, core_r, uu_s, uu_r, ud_s, ud_r, um_s, um_r,
         ph_s, ph_r, r1_s, r1_r, r2_s, r2_r, out_s, out_r, qc_s, qc_r,
         qb_s, qb_r, qz_s, qz_r,
     ) = refs[4 + PARTS :]
@@ -259,8 +249,7 @@
     kw, width = u_ref.shape
     sub = kw // PARTS
     rows_here, cols_here = a_ref.shape
-    slots = slot_ref.shape[1]
-    chosen = slots * BLK
+    slots = cols_here // BLK // 2
     rq = rows_here // cols
     hq = rq // 2
     wq = width // cols
@@ -351,13 +340,19 @@
                     start(unit_copy(source, chip, d, up), onward)
             start(unit_mate(source), (source >= 0) & (source < rows))
 
-    for h in range(PARTS):
-        gathered[h][c] = pt_ref[part(h), :]
+    inputs = [
+        pltpu.make_async_copy(pt_ref.at[part(h), :], gathered[h].at[c], in_sem.at[h])
+        for h in range(PARTS)
+    ]
+    inputs.append(pltpu.make_async_copy(u_ref, unit_own, in_sem.at[PARTS]))
+    inputs.append(pltpu.make_async_copy(pivot_hbm, pivot_ref, in_sem.at[PARTS + 1]))
+    for copy in inputs:
+        copy.start()
 
     def prepare(t):
         a_copy(t).wait()
         for s in range(slots):
-            column = slot_ref[2, s] * BLK
+            column = table_ref[2 * slots + s] * BLK
             high, low = halves(stage[t % 2][:, pl.ds(column, BLK)])
             a_high[pl.ds(t * tile_rows, tile_rows), s * BLK : (s + 1) * BLK] = high
             a_low[pl.ds(t * tile_rows, tile_rows), s * BLK : (s + 1) * BLK] = low
@@ -377,10 +372,11 @@
     def own_part(h):
         for i in range(cols - 1):
             own_copy(h, i, plane[i]).wait_recv()
+        inputs[h].wait()
         for s in range(slots):
-            offset = slot_ref[1, s] * BLK
-            value = gathered[h][slot_ref[0, s], :, pl.ds(offset, BLK)]
-            pt[r, part(h), s * BLK : (s + 1) * BLK] = value * live_ref[s]
+            offset = table_ref[slots + s] * BLK
+            value = gathered[h][table_ref[s], :, pl.ds(offset, BLK)]
+            pt[r, part(h), s * BLK : (s + 1) * BLK] = value * table_ref[3 * slots + s].astype(jnp.float32)
         start(z_copy(r, h, 0, True), z < nz - 1)
         start(z_copy(r, h, 0, False), z > 0)
         start(core_copy(r, h))
@@ -472,11 +468,11 @@
     def listed_part(h):
         for target in range(rows):
             for k in range(quarter):
-                at = target * quarter + k
-                offset = block_ref[1, at] * BLK
-                value = gathered[h][block_ref[0, at], :, pl.ds(offset, BLK)]
+                at = 4 * slots + 3 * (target * quarter + k)
+                offset = table_ref[at + 1] * BLK
+                value = gathered[h][table_ref[at], :, pl.ds(offset, BLK)]
                 ph_send[target, part(h), k * BLK : (k + 1) * BLK] = (
-                    value * live_ref[slots + at]
+                    value * table_ref[at + 2].astype(jnp.float32)
                 )
 
     def listed_send():
@@ -490,7 +486,8 @@
         ph_recv[r] = ph_send[r]
 
     def turn_unit():
-        uf[r] = u_ref[...]
+        inputs[PARTS].wait()
+        uf[r] = unit_own[...]
         for chip in range(nz):
             unit_mate(2 * chip + 1 - p).wait_recv()
         for chip in range(nz):
@@ -568,6 +565,7 @@
         total = qd[z]
         for step in range(1, nz):
             total = total + qz[step]
+        inputs[PARTS + 1].wait()
         diag_ref[...] = pivot_ref[...] - total
 
     def finish():
@@ -638,7 +636,7 @@
     stored, kw = panel.shape
     width = unit_inverse.shape[1]
     row_blocks, range_blocks = rows_here // BLK, cols_here // BLK
-    slot_ids, block_ids, live = tables(panel_blocks, cols, range_blocks, row_blocks, rows)
+    table = tables(panel_blocks, cols, range_blocks, row_blocks, rows)
     slots = range_blocks // 2
     chosen = slots * BLK
     nz = rows // 2
@@ -672,6 +670,9 @@
             pltpu.VMEM((cols - 1, nz, kw, wq), f32),
             pltpu.VMEM((nz, kw, wq), f32),
             pltpu.VMEM((nz, kw, wq), f32),
+            pltpu.VMEM(unit_inverse.shape, f32),
+            pltpu.VMEM(pivot_inverse.shape, f32),
+            dma((PARTS + 2,)),
             dma((2,)),
             dma((PARTS, cols - 1)),
             dma((PARTS, cols - 1)),
@@ -709,13 +710,13 @@
             jax.ShapeDtypeStruct((wq, rows_here), f32),
             jax.ShapeDtypeStruct(pivot_inverse.shape, f32),
         ),
-        in_specs=[smem, smem, smem, vmem, vmem, vmem, pl.BlockSpec(memory_space=pl.ANY)],
+        in_specs=[smem] + [pl.BlockSpec(memory_space=pltpu.HBM)] * 4,
         out_specs=(vmem, vmem),
         scratch_shapes=scratch,
         compiler_params=pltpu.CompilerParams(
             collective_id=0, has_side_effects=True, vmem_limit_bytes=50 << 20
         ),
-    )(slot_ids, block_ids, live, panel.T, unit_inverse, pivot_inverse, ancestor_inverse)
+    )(table, panel.T, unit_inverse, pivot_inverse, ancestor_inverse)
 
 
 def fits(mesh, ancestor_inverse, panel, unit_inverse):

time: 90.6 us -> 88.7 us (0.979)
  local copies, waits for them, and re-layouts: 6.09 us -> 4.79 us
    unnamed x14 -> x10, local copies, waits for them, and re-layouts: 6.09 us -> 4.79 us
where the time goes in v4:
time: 88.7 us; the launch traced here: 88.3 us
  Pallas kernels  82.8 us (93%)
  local copies, waits for them, and re-layouts  4.79 us (5%)
    pallas_call x1, Pallas kernels, fused(): pl.pallas_call(functools.partial(fused_kernel, rows, cols), out_shape=(ja...  80.2 us
    unnamed x10, local copies, waits for them, and re-layouts  4.79 us
    pallas_call x1, Pallas kernels, tables(): pl.pallas_call(functools.partial(table_kernel, cols, range_blocks, row_bl...  2.59 us

profile of v4, /device:TPU:0, one launch (start us, length us, event | category | flops | bytes accessed | tf_op | source)
XLA Modules:
  0.0 88.3 jit_solution(3454214027151417513)
XLA Ops:
  0.6 2.6 %shard_map.68.table_ref = s32[120]{0:T(128)} custom-call(s32[44]{0:T(128)} %ids_ref.1), custom_call_target="tpu_custom_call" | custom-call | tf_op jit(solution)/shard_map/pallas_call | solution.py:202
  3.2 0.0 copy-start
  3.2 1.0 %copy-done = f32[1408,64]{0,1:T(8,128)S(1)} copy-done((f32[1408,64]{0,1:T(8,128)S(1)}, f32[1408,64]{0,1:T(8,128)}, u32[]{:S(2)}) %copy-start) | copy-done | bytes 360472
  4.2 0.0 copy-start.1
  4.2 0.9 %copy-done.1 = f32[64,512]{1,0:T(8,128)S(1)} copy-done((f32[64,512]{1,0:T(8,128)S(1)}, f32[64,512]{1,0:T(8,128)}, u32[]{:S(2)}) %copy-start.1) | copy-done | bytes 131096
  5.1 0.0 copy-start.2
  5.1 0.8 copy-done.2
  5.9 0.0 copy-start.3
  5.9 0.7 copy-done.3
  6.5 80.2 %shard_map.69 = (f32[128,1536]{1,0:T(8,128)S(1)}, f32[64,128]{1,0:T(8,128)S(1)}) custom-call(s32[120]{0:T(128)S(1)} %copy-done.3, f32[64,1408]{1,0:T(8,128)S(1)} %bitcast.1, f32[64,512]{1,0:T(8,128)S(1)} %copy-done.1, f32[64,128]{1,0:T(8,128)S(1)} %copy-done.2, f32[1536,3072]{1,0:T(8,128)} %a_ref.1), custom_call_target="tpu_custom_call" | custom-call | tf_op jit(solution)/shard_map/pallas_call | solution.py:707
  86.8 0.9 copy.9
  87.6 0.6 copy.10
Async XLA Ops:
  3.2 1.0 %copy-start = (f32[1408,64]{0,1:T(8,128)S(1)}, f32[1408,64]{0,1:T(8,128)}, u32[]{:S(2)}) copy-start(f32[1408,64]{0,1:T(8,128)} %param.6) | copy-start | bytes 1081348
  4.2 0.9 %copy-start.1 = (f32[64,512]{1,0:T(8,128)S(1)}, f32[64,512]{1,0:T(8,128)}, u32[]{:S(2)}) copy-start(f32[64,512]{1,0:T(8,128)} %u_ref.1) | copy-start | bytes 393220
  5.1 0.8 copy-start.2
  5.9 0.7 copy-start.3
